TPU v7x, 32 devices: a whole 2x2x4 slice. The times are simulated.
32 devices in a mesh: grp: 4 (over y, core), blk: 8 (over z, x).
Axes of the slice: x: 2, y: 2, z: 4, core: 2. Of those that a mesh axis runs over, the one named last changes fastest.
Arguments:
- queries: bfloat16 [4, 128, 4096], P(None, ('blk', 'grp')), may hold values from -24 to 24
- cache_keys: bfloat16 [4, 3584, 512], P('grp', 'blk'), may hold values from -24 to 24
- cache_values: bfloat16 [4, 3584, 512], P('grp', 'blk'), may hold values from -15 to 15
- new_keys: bfloat16 [4, 128, 512], P(None, ('blk', 'grp')), may hold values from -6 to 6
- new_values: bfloat16 [4, 128, 512], P(None, ('blk', 'grp')), may hold values from -15 to 15
- hits: int32 [4], P('grp'), may hold values from 448 to 3584, as said below
- counts: int32 [4], P('grp'), may hold values from 64 to 128, as said below
- assign: int32 [4, 8], P('grp'), may hold values from 0 to 7, each once within a row
Outputs:
- attended: bfloat16 [4, 128, 4096], P(None, ('blk', 'grp'))
Inputs may be any that keep to these rules, and one draw needn't show every extreme that they name: Cached positions of request r below hits[r] are valid; in every draw some request has all 3584 valid. New tokens of request r at order counts[r] or later are padding; in every draw some request has all 128.
All inputs are finite; a program needn't handle non-finite values.
Results may differ from a plain program's by a relative error of at most 0.0085.
Values may be sent and summed in bfloat16 or wider, within the bound.
A program may use at most 128 MiB of HBM per device.

v0:
```python
import jax
import jax.numpy as jnp
from jax import lax
from jax.sharding import PartitionSpec as P

HEAD_DIM = 128


def shifted(value, axis, by):
    length = lax.axis_size(axis)
    return lax.ppermute(value, axis, [(i, (i + by) % length) for i in range(length)])


def partial_block(queries, keys, values, allowed, kv_heads):
    row_count, full_width = queries.shape
    key_count = keys.shape[0]
    head_dim = keys.shape[1] // kv_heads
    group_size = full_width // head_dim // kv_heads
    query_heads = queries.reshape(row_count, kv_heads, group_size, head_dim)
    key_heads = keys.reshape(key_count, kv_heads, head_dim)
    scores = jnp.einsum(
        "qkgd,nkd->kgqn", query_heads, key_heads, preferred_element_type=jnp.float32
    ) * head_dim ** (-0.5)
    scores = jnp.where(allowed[None, None], scores, -1e30)
    block_max = jnp.max(scores, axis=-1)
    exp_terms = jnp.where(allowed[None, None], jnp.exp(scores - block_max[..., None]), 0.0)
    weight_sum = jnp.sum(exp_terms, axis=-1)
    prob_bf = exp_terms.astype(jnp.bfloat16)
    value_heads = values.reshape(key_count, kv_heads, head_dim)
    blended = jnp.einsum("kgqn,nkd->qkgd", prob_bf, value_heads, preferred_element_type=jnp.float32)
    floor_sum = jnp.maximum(weight_sum, 1.0).transpose(2, 0, 1)[..., None]
    blended = (blended / floor_sum).reshape(row_count, full_width).astype(jnp.bfloat16)
    maxima = block_max.transpose(2, 0, 1).reshape(row_count, -1)
    weights = weight_sum.transpose(2, 0, 1).reshape(row_count, -1)
    return (blended, maxima, weights)


def combine(running, part, head_count):
    summed, maxima, weights = running
    blended, part_max, part_weight = part
    row_count, full_width = summed.shape
    highest = jnp.maximum(maxima, part_max)
    old_scale = jnp.exp(maxima - highest)
    new_scale = part_weight * jnp.exp(part_max - highest)
    summed = summed.reshape(row_count, head_count, -1) * old_scale[:, :, None]
    summed = summed + new_scale[:, :, None] * blended.astype(jnp.float32).reshape(
        row_count, head_count, -1
    )
    return (summed.reshape(row_count, full_width), highest, weights * old_scale + new_scale)


def local(queries, cache_keys, cache_values, new_keys, new_values, hits, counts, assign):
    local_q, local_k, local_v = (
        lax.all_to_all(queries, "grp", split_axis=0, concat_axis=1, tiled=True),
        lax.all_to_all(new_keys, "grp", split_axis=0, concat_axis=1, tiled=True),
        lax.all_to_all(new_values, "grp", split_axis=0, concat_axis=1, tiled=True),
    )
    local_q = local_q[0]
    local_k = local_k[0]
    local_v = local_v[0]
    row_count, full_width = local_q.shape
    kv_width = local_k.shape[1]
    cached = cache_keys.shape[1]
    head_count = full_width // HEAD_DIM
    kv_heads = kv_width // HEAD_DIM
    hit_limit = hits[0]
    filled = counts[0]
    block_order = assign[0]
    cycle_index = lax.axis_index("blk")
    members = lax.axis_size("blk")
    query_lane = jnp.arange(row_count, dtype=jnp.int32)
    cache_lane = jnp.arange(cached, dtype=jnp.int32)
    own_pos = block_order[cycle_index] * row_count + query_lane
    block_keys = jnp.concatenate([cache_keys[0], local_k], 0)
    block_values = jnp.concatenate([cache_values[0], local_v], 0)

    def allowed_for(block_index, query_pos):
        cache_ok = block_index * cached + cache_lane < hit_limit
        fresh_ok = (block_order[block_index] * row_count + query_lane)[None, :] <= query_pos[
            :, None
        ]
        return jnp.concatenate(
            [jnp.broadcast_to(cache_ok[None, :], (query_pos.shape[0], cached)), fresh_ok], 1
        )

    start = (
        jnp.zeros((row_count, full_width), jnp.float32),
        jnp.full((row_count, head_count), -1e30, jnp.float32),
        jnp.zeros((row_count, head_count), jnp.float32),
    )

    def pass_state(running):
        return shifted(running, "blk", 1)

    def visit_block(visitor, running, turn_index):
        source = (cycle_index - turn_index) % members
        query_pos = block_order[source] * row_count + query_lane
        part = partial_block(
            visitor, block_keys, block_values, allowed_for(cycle_index, query_pos), kv_heads
        )
        return pass_state(combine(running, part, head_count))

    def cycle_turn(turn_index, loop_state):
        visitor, running = loop_state
        running = visit_block(visitor, running, turn_index)
        visitor = shifted(visitor, "blk", 1)
        return (visitor, running)

    visitor, running = lax.fori_loop(0, members - 1, cycle_turn, (local_q, start))
    running = visit_block(visitor, running, members - 1)
    summed, maxima, weights = running
    blended = (summed.reshape(row_count, head_count, -1) / weights[:, :, None]).reshape(
        row_count, full_width
    )
    blended = jnp.where((own_pos < filled)[:, None], blended, 0.0).astype(jnp.bfloat16)
    return lax.all_to_all(blended[None], "grp", split_axis=1, concat_axis=0, tiled=True)


def solution(mesh):
    return jax.shard_map(
        local,
        mesh=mesh,
        in_specs=(
            P(None, ("blk", "grp"), None),
            P("grp", "blk", None),
            P("grp", "blk", None),
            P(None, ("blk", "grp"), None),
            P(None, ("blk", "grp"), None),
            P("grp"),
            P("grp"),
            P("grp", None),
        ),
        out_specs=P(None, ("blk", "grp"), None),
        check_vma=False,
    )
```

profile of v0, /device:TPU:0, one launch (start us, length us, event | category | flops | bytes accessed | tf_op | source)
XLA Modules:
  0.0 164.6 jit_solution(10242938498501873092)
XLA Ops:
  0.0 4.3 %all-to-all-start.1 = ((bf16[4,4,512]{2,1,0:T(4,128)(2,1)}), bf16[4,4,512]{2,1,0:T(4,128)(2,1)S(1)}, u32[]{:S(2)}, u32[]{:S(2)}) async-start(bf16[4,4,512]{2,1,0:T(4,128)(2,1)} %param.13), calls=%async_computation.1 | async-start | bytes 32768 | tf_op jit(solution)/shard_map/all_to_all | solution.py:55
  4.3 0.7 copy-done.5
  4.9 0.6 constant_dynamic-slice_fusion
  7.6 1.1 concatenate.36
  8.7 0.9 copy.55
  10.0 3.4 %all-to-all-start.2 = ((bf16[4,4,512]{2,1,0:T(4,128)(2,1)}), bf16[4,4,512]{2,1,0:T(4,128)(2,1)S(1)}, u32[]{:S(2)}, u32[]{:S(2)}) async-start(bf16[4,4,512]{2,1,0:T(4,128)(2,1)} %param.14), calls=%async_computation.2 | async-start | bytes 32768 | tf_op jit(solution)/shard_map/all_to_all | solution.py:56
  13.7 3.7 %all-to-all-done.2 = bf16[4,4,512]{2,1,0:T(4,128)(2,1)S(1)} async-done(((bf16[4,4,512]{2,1,0:T(4,128)(2,1)}), bf16[4,4,512]{2,1,0:T(4,128)(2,1)S(1)}, u32[]{:S(2)}, u32[]{:S(2)}) %all-to-all-start.2) | async-done | bytes 16416 | tf_op jit(solution)/shard_map/all_to_all | solution.py:56
  17.3 3.3 %all-to-all-start = ((bf16[4,4,4096]{2,1,0:T(4,128)(2,1)}), bf16[4,4,4096]{2,1,0:T(4,128)(2,1)S(1)}, u32[]{:S(2)}, u32[]{:S(2)}) async-start(bf16[4,4,4096]{2,1,0:T(4,128)(2,1)} %param.10), calls=%async_computation | async-start | bytes 262144 | tf_op jit(solution)/shard_map/all_to_all | solution.py:54
  20.8 0.6 copy-done.1
  21.6 3.7 %all-to-all-done = bf16[4,4,4096]{2,1,0:T(4,128)(2,1)S(1)} async-done(((bf16[4,4,4096]{2,1,0:T(4,128)(2,1)}), bf16[4,4,4096]{2,1,0:T(4,128)(2,1)S(1)}, u32[]{:S(2)}, u32[]{:S(2)}) %all-to-all-start) | async-done | bytes 131104 | tf_op jit(solution)/shard_map/all_to_all | solution.py:54
  25.3 115.3 %while.24 = (s32[]{:T(128)}, bf16[16,4096]{1,0:T(8,128)(2,1)S(1)}, f32[16,4096]{1,0:T(8,128)S(1)}, f32[16,32]{0,1:T(8,128)S(1)}, f32[16,32]{0,1:T(8,128)S(1)}, /...) while((s32[]{:T(128)}, bf16[16,4096]{1,0:T(8,128)(2,1)S(1)}, ...), condition=%wide.wide.region_3.4_spmd.clone.clone, body=%wide.wide.region_0.3_spmd.clone.clone.sunk | while | flops 124177328 | bytes 8742969 | solution.py:109
  25.4 0.7 dynamic_slice.32
  26.8 0.7 fusion.68
  27.6 0.4 fusion.69
  29.3 0.5 fusion.72
  29.7 2.0 %collective-permute-start.1 = (f32[16,4096]{1,0:T(8,128)S(1)}, f32[16,4096]{1,0:T(8,128)S(1)}, u32[]{:S(2)}, u32[]{:S(2)}) collective-permute-start(f32[16,4096]{1,0:T(8,128)S(1)} %fusion.72), channel_id=1, source_target_pairs={{0,1},{1,2},{2,3},{3,4},{4,5},{5,6},{6,7},{7,0},{8,9},{9,10},{10,1... | collective-permute-start | bytes 786440 | tf_op jit(solution)/shard_map/while/body/eval_jaxpr/ppermute | solution.py:11
  31.7 1.5 collective-permute-start
  33.3 1.5 collective-permute-start.2
  34.8 1.5 collective-permute-start.3
  36.3 7.7 %collective-permute-done.2 = f32[16,32]{0,1:T(8,128)S(1)} collective-permute-done((f32[16,32]{0,1:T(8,128)S(1)}, f32[16,32]{0,1:T(8,128)S(1)}, u32[]{:S(2)}, u32[]{:S(2)}) %collective-permute-start.2) | collective-permute-done | bytes 2080 | tf_op jit(solution)/shard_map/while/body/eval_jaxpr/ppermute | solution.py:11
  44.3 0.7 dynamic_slice.32
  45.7 0.7 fusion.68
  46.4 0.4 fusion.69
  48.1 0.5 fusion.72
  48.7 1.1 collective-permute-start
  49.8 0.6 collective-permute-start.2
  50.4 2.5 %collective-permute-start.3 = (f32[16,32]{0,1:T(8,128)S(1)}, f32[16,32]{0,1:T(8,128)S(1)}, u32[]{:S(2)}, u32[]{:S(2)}) collective-permute-start(f32[16,32]{0,1:T(8,128)S(1)} %get-tuple-element.565), channel_id=1, source_target_pairs={{0,1},{1,2},{2,3},{3,4},{4,5},{5,6},{6,7},{7,0},{8,9},{9,10},{10,1... | collective-permute-start | bytes 6152 | tf_op jit(solution)/shard_map/while/body/eval_jaxpr/ppermute | solution.py:11
  52.8 8.9 %collective-permute-done.2 = f32[16,32]{0,1:T(8,128)S(1)} collective-permute-done((f32[16,32]{0,1:T(8,128)S(1)}, f32[16,32]{0,1:T(8,128)S(1)}, u32[]{:S(2)}, u32[]{:S(2)}) %collective-permute-start.2) | collective-permute-done | bytes 2080 | tf_op jit(solution)/shard_map/while/body/eval_jaxpr/ppermute | solution.py:11
  62.0 0.7 dynamic_slice.32
  63.4 0.7 fusion.68
  64.2 0.4 fusion.69
  65.9 0.5 fusion.72
  66.5 2.0 %collective-permute-start.3 = (f32[16,32]{0,1:T(8,128)S(1)}, f32[16,32]{0,1:T(8,128)S(1)}, u32[]{:S(2)}, u32[]{:S(2)}) collective-permute-start(f32[16,32]{0,1:T(8,128)S(1)} %get-tuple-element.565), channel_id=1, source_target_pairs={{0,1},{1,2},{2,3},{3,4},{4,5},{5,6},{6,7},{7,0},{8,9},{9,10},{10,1... | collective-permute-start | bytes 6152 | tf_op jit(solution)/shard_map/while/body/eval_jaxpr/ppermute | solution.py:11
  68.5 10.2 %collective-permute-done.2 = f32[16,32]{0,1:T(8,128)S(1)} collective-permute-done((f32[16,32]{0,1:T(8,128)S(1)}, f32[16,32]{0,1:T(8,128)S(1)}, u32[]{:S(2)}, u32[]{:S(2)}) %collective-permute-start.2) | collective-permute-done | bytes 2080 | tf_op jit(solution)/shard_map/while/body/eval_jaxpr/ppermute | solution.py:11
  78.9 0.7 dynamic_slice.32
  80.3 0.7 fusion.68
  81.1 0.4 fusion.69
  82.8 0.5 fusion.72
  83.5 11.2 %collective-permute-done.2 = f32[16,32]{0,1:T(8,128)S(1)} collective-permute-done((f32[16,32]{0,1:T(8,128)S(1)}, f32[16,32]{0,1:T(8,128)S(1)}, u32[]{:S(2)}, u32[]{:S(2)}) %collective-permute-start.2) | collective-permute-done | bytes 2080 | tf_op jit(solution)/shard_map/while/body/eval_jaxpr/ppermute | solution.py:11
  95.0 0.7 dynamic_slice.32
  96.3 0.7 fusion.68
  97.1 0.4 fusion.69
  98.8 0.5 fusion.72
  99.5 0.5 collective-permute-start.3
  100.0 10.0 %collective-permute-done.2 = f32[16,32]{0,1:T(8,128)S(1)} collective-permute-done((f32[16,32]{0,1:T(8,128)S(1)}, f32[16,32]{0,1:T(8,128)S(1)}, u32[]{:S(2)}, u32[]{:S(2)}) %collective-permute-start.2) | collective-permute-done | bytes 2080 | tf_op jit(solution)/shard_map/while/body/eval_jaxpr/ppermute | solution.py:11
  110.2 0.7 dynamic_slice.32
  111.6 0.7 fusion.68
  112.4 0.4 fusion.69
  114.1 0.5 fusion.72
  114.7 1.3 collective-permute-start.3
  116.0 9.2 %collective-permute-done.2 = f32[16,32]{0,1:T(8,128)S(1)} collective-permute-done((f32[16,32]{0,1:T(8,128)S(1)}, f32[16,32]{0,1:T(8,128)S(1)}, u32[]{:S(2)}, u32[]{:S(2)}) %collective-permute-start.2) | collective-permute-done | bytes 2080 | tf_op jit(solution)/shard_map/while/body/eval_jaxpr/ppermute | solution.py:11
  125.5 0.7 dynamic_slice.32
  126.9 0.7 fusion.68
  129.3 0.5 fusion.72
  130.0 1.3 collective-permute-start.3
  131.3 9.2 %collective-permute-done.2 = f32[16,32]{0,1:T(8,128)S(1)} collective-permute-done((f32[16,32]{0,1:T(8,128)S(1)}, f32[16,32]{0,1:T(8,128)S(1)}, u32[]{:S(2)}, u32[]{:S(2)}) %collective-permute-start.2) | collective-permute-done | bytes 2080 | tf_op jit(solution)/shard_map/while/body/eval_jaxpr/ppermute | solution.py:11
  140.7 0.4 fusion.51
  142.4 0.5 fusion.39
  143.7 8.5 %collective-permute-done.5 = f32[16,32]{0,1:T(8,128)S(1)} collective-permute-done((f32[16,32]{0,1:T(8,128)S(1)}, f32[16,32]{0,1:T(8,128)S(1)}, u32[]{:S(2)}, u32[]{:S(2)}) %collective-permute-start.5) | collective-permute-done | bytes 2080 | tf_op jit(solution)/shard_map/ppermute | solution.py:11
  152.8 0.5 broadcast.135
  153.3 1.4 reduce.2
  154.9 8.2 %all_to_all.19 = bf16[4,2,8192]{2,1,0:T(2,128)(2,1)S(1)} all-to-all(bf16[4,2,8192]{2,1,0:T(2,128)(2,1)S(1)} %reshape.215), channel_id=1, replica_groups=mesh['grp'=4,'blk'=8] {'grp'}, dimensions={0} | all-to-all | bytes 262144 | tf_op jit(solution)/shard_map/all_to_all | solution.py:116
  163.2 0.7 bitcast_reduce_fusion
  163.9 0.7 all_to_all.14
  (203 shorter events, 15.9 us)
Async XLA Ops:
  0.0 10.0 %all-to-all-start.1 = ((bf16[4,4,512]{2,1,0:T(4,128)(2,1)}), bf16[4,4,512]{2,1,0:T(4,128)(2,1)S(1)}, u32[]{:S(2)}, u32[]{:S(2)}) async-start(bf16[4,4,512]{2,1,0:T(4,128)(2,1)} %param.13), calls=%async_computation.1 | async-start | bytes 32768 | tf_op jit(solution)/shard_map/all_to_all | solution.py:55
  4.3 0.7 copy-start.5
  8.7 1.1 copy-start.3
  9.9 3.5 %copy-start.2 = (bf16[1,448,512]{2,1,0:T(8,128)(2,1)S(1)}, bf16[1,448,512]{2,1,0:T(8,128)(2,1)}, u32[]{:S(2)}) copy-start(bf16[1,448,512]{2,1,0:T(8,128)(2,1)} %param.11) | copy-start | bytes 1376260
  10.0 7.3 %all-to-all-start.2 = ((bf16[4,4,512]{2,1,0:T(4,128)(2,1)}), bf16[4,4,512]{2,1,0:T(4,128)(2,1)S(1)}, u32[]{:S(2)}, u32[]{:S(2)}) async-start(bf16[4,4,512]{2,1,0:T(4,128)(2,1)} %param.14), calls=%async_computation.2 | async-start | bytes 32768 | tf_op jit(solution)/shard_map/all_to_all | solution.py:56
  13.5 3.8 %copy-start = (bf16[464,512]{1,0:T(8,128)(2,1)}, bf16[464,512]{1,0:T(8,128)(2,1)S(1)}, u32[]{:S(2)}) copy-start(bf16[464,512]{1,0:T(8,128)(2,1)S(1)} %pad_maximum_fusion) | copy-start | bytes 1425412
  17.3 7.9 %all-to-all-start = ((bf16[4,4,4096]{2,1,0:T(4,128)(2,1)}), bf16[4,4,4096]{2,1,0:T(4,128)(2,1)S(1)}, u32[]{:S(2)}, u32[]{:S(2)}) async-start(bf16[4,4,4096]{2,1,0:T(4,128)(2,1)} %param.10), calls=%async_computation | async-start | bytes 262144 | tf_op jit(solution)/shard_map/all_to_all | solution.py:54
  20.7 0.8 copy-start.1
  25.3 115.4 %copy-start.4 = (bf16[448,4,128]{2,0,1:T(8,128)(2,1)S(1)}, bf16[448,4,128]{2,0,1:T(8,128)(2,1)}, u32[]{:S(2)}) copy-start(bf16[448,4,128]{2,0,1:T(8,128)(2,1)} %copy.55) | copy-start | bytes 1376260
  29.7 14.5 %collective-permute-start.1 = (f32[16,4096]{1,0:T(8,128)S(1)}, f32[16,4096]{1,0:T(8,128)S(1)}, u32[]{:S(2)}, u32[]{:S(2)}) collective-permute-start(f32[16,4096]{1,0:T(8,128)S(1)} %fusion.72), channel_id=1, source_target_pairs={{0,1},{1,2},{2,3},{3,4},{4,5},{5,6},{6,7},{7,0},{8,9},{9,10},{10,1... | collective-permute-start | bytes 786440 | tf_op jit(solution)/shard_map/while/body/eval_jaxpr/ppermute | solution.py:11
  31.7 12.5 %collective-permute-start = (bf16[16,4096]{1,0:T(8,128)(2,1)S(1)}, bf16[16,4096]{1,0:T(8,128)(2,1)S(1)}, u32[]{:S(2)}, u32[]{:S(2)}) collective-permute-start(bf16[16,4096]{1,0:T(8,128)(2,1)S(1)} %copy.144), channel_id=1, source_target_pairs={{0,1},{1,2},{2,3},{3,4},{4,5},{5,6},{6,7},{7,0},{8,9},{9,10},{10,1... | collective-permute-start | bytes 393224 | tf_op jit(solution)/shard_map/while/body/eval_jaxpr/ppermute | solution.py:11
  33.3 10.8 %collective-permute-start.2 = (f32[16,32]{0,1:T(8,128)S(1)}, f32[16,32]{0,1:T(8,128)S(1)}, u32[]{:S(2)}, u32[]{:S(2)}) collective-permute-start(f32[16,32]{0,1:T(8,128)S(1)} %get-tuple-element.564), channel_id=1, source_target_pairs={{0,1},{1,2},{2,3},{3,4},{4,5},{5,6},{6,7},{7,0},{8,9},{9,10},{10,1... | collective-permute-start | bytes 6152 | tf_op jit(solution)/shard_map/while/body/eval_jaxpr/ppermute | solution.py:11
  34.8 9.4 %collective-permute-start.3 = (f32[16,32]{0,1:T(8,128)S(1)}, f32[16,32]{0,1:T(8,128)S(1)}, u32[]{:S(2)}, u32[]{:S(2)}) collective-permute-start(f32[16,32]{0,1:T(8,128)S(1)} %get-tuple-element.565), channel_id=1, source_target_pairs={{0,1},{1,2},{2,3},{3,4},{4,5},{5,6},{6,7},{7,0},{8,9},{9,10},{10,1... | collective-permute-start | bytes 6152 | tf_op jit(solution)/shard_map/while/body/eval_jaxpr/ppermute | solution.py:11
  48.6 13.4 %collective-permute-start.1 = (f32[16,4096]{1,0:T(8,128)S(1)}, f32[16,4096]{1,0:T(8,128)S(1)}, u32[]{:S(2)}, u32[]{:S(2)}) collective-permute-start(f32[16,4096]{1,0:T(8,128)S(1)} %fusion.72), channel_id=1, source_target_pairs={{0,1},{1,2},{2,3},{3,4},{4,5},{5,6},{6,7},{7,0},{8,9},{9,10},{10,1... | collective-permute-start | bytes 786440 | tf_op jit(solution)/shard_map/while/body/eval_jaxpr/ppermute | solution.py:11
  48.7 13.3 %collective-permute-start = (bf16[16,4096]{1,0:T(8,128)(2,1)S(1)}, bf16[16,4096]{1,0:T(8,128)(2,1)S(1)}, u32[]{:S(2)}, u32[]{:S(2)}) collective-permute-start(bf16[16,4096]{1,0:T(8,128)(2,1)S(1)} %copy.144), channel_id=1, source_target_pairs={{0,1},{1,2},{2,3},{3,4},{4,5},{5,6},{6,7},{7,0},{8,9},{9,10},{10,1... | collective-permute-start | bytes 393224 | tf_op jit(solution)/shard_map/while/body/eval_jaxpr/ppermute | solution.py:11
  49.8 12.0 %collective-permute-start.2 = (f32[16,32]{0,1:T(8,128)S(1)}, f32[16,32]{0,1:T(8,128)S(1)}, u32[]{:S(2)}, u32[]{:S(2)}) collective-permute-start(f32[16,32]{0,1:T(8,128)S(1)} %get-tuple-element.564), channel_id=1, source_target_pairs={{0,1},{1,2},{2,3},{3,4},{4,5},{5,6},{6,7},{7,0},{8,9},{9,10},{10,1... | collective-permute-start | bytes 6152 | tf_op jit(solution)/shard_map/while/body/eval_jaxpr/ppermute | solution.py:11
  50.4 11.6 %collective-permute-start.3 = (f32[16,32]{0,1:T(8,128)S(1)}, f32[16,32]{0,1:T(8,128)S(1)}, u32[]{:S(2)}, u32[]{:S(2)}) collective-permute-start(f32[16,32]{0,1:T(8,128)S(1)} %get-tuple-element.565), channel_id=1, source_target_pairs={{0,1},{1,2},{2,3},{3,4},{4,5},{5,6},{6,7},{7,0},{8,9},{9,10},{10,1... | collective-permute-start | bytes 6152 | tf_op jit(solution)/shard_map/while/body/eval_jaxpr/ppermute | solution.py:11
  66.3 12.5 %collective-permute-start.1 = (f32[16,4096]{1,0:T(8,128)S(1)}, f32[16,4096]{1,0:T(8,128)S(1)}, u32[]{:S(2)}, u32[]{:S(2)}) collective-permute-start(f32[16,4096]{1,0:T(8,128)S(1)} %fusion.72), channel_id=1, source_target_pairs={{0,1},{1,2},{2,3},{3,4},{4,5},{5,6},{6,7},{7,0},{8,9},{9,10},{10,1... | collective-permute-start | bytes 786440 | tf_op jit(solution)/shard_map/while/body/eval_jaxpr/ppermute | solution.py:11
  66.4 12.4 %collective-permute-start = (bf16[16,4096]{1,0:T(8,128)(2,1)S(1)}, bf16[16,4096]{1,0:T(8,128)(2,1)S(1)}, u32[]{:S(2)}, u32[]{:S(2)}) collective-permute-start(bf16[16,4096]{1,0:T(8,128)(2,1)S(1)} %copy.144), channel_id=1, source_target_pairs={{0,1},{1,2},{2,3},{3,4},{4,5},{5,6},{6,7},{7,0},{8,9},{9,10},{10,1... | collective-permute-start | bytes 393224 | tf_op jit(solution)/shard_map/while/body/eval_jaxpr/ppermute | solution.py:11
  66.5 12.2 %collective-permute-start.2 = (f32[16,32]{0,1:T(8,128)S(1)}, f32[16,32]{0,1:T(8,128)S(1)}, u32[]{:S(2)}, u32[]{:S(2)}) collective-permute-start(f32[16,32]{0,1:T(8,128)S(1)} %get-tuple-element.564), channel_id=1, source_target_pairs={{0,1},{1,2},{2,3},{3,4},{4,5},{5,6},{6,7},{7,0},{8,9},{9,10},{10,1... | collective-permute-start | bytes 6152 | tf_op jit(solution)/shard_map/while/body/eval_jaxpr/ppermute | solution.py:11
  66.5 12.3 %collective-permute-start.3 = (f32[16,32]{0,1:T(8,128)S(1)}, f32[16,32]{0,1:T(8,128)S(1)}, u32[]{:S(2)}, u32[]{:S(2)}) collective-permute-start(f32[16,32]{0,1:T(8,128)S(1)} %get-tuple-element.565), channel_id=1, source_target_pairs={{0,1},{1,2},{2,3},{3,4},{4,5},{5,6},{6,7},{7,0},{8,9},{9,10},{10,1... | collective-permute-start | bytes 6152 | tf_op jit(solution)/shard_map/while/body/eval_jaxpr/ppermute | solution.py:11
  83.2 11.7 %collective-permute-start.1 = (f32[16,4096]{1,0:T(8,128)S(1)}, f32[16,4096]{1,0:T(8,128)S(1)}, u32[]{:S(2)}, u32[]{:S(2)}) collective-permute-start(f32[16,4096]{1,0:T(8,128)S(1)} %fusion.72), channel_id=1, source_target_pairs={{0,1},{1,2},{2,3},{3,4},{4,5},{5,6},{6,7},{7,0},{8,9},{9,10},{10,1... | collective-permute-start | bytes 786440 | tf_op jit(solution)/shard_map/while/body/eval_jaxpr/ppermute | solution.py:11
  83.3 11.6 %collective-permute-start = (bf16[16,4096]{1,0:T(8,128)(2,1)S(1)}, bf16[16,4096]{1,0:T(8,128)(2,1)S(1)}, u32[]{:S(2)}, u32[]{:S(2)}) collective-permute-start(bf16[16,4096]{1,0:T(8,128)(2,1)S(1)} %copy.144), channel_id=1, source_target_pairs={{0,1},{1,2},{2,3},{3,4},{4,5},{5,6},{6,7},{7,0},{8,9},{9,10},{10,1... | collective-permute-start | bytes 393224 | tf_op jit(solution)/shard_map/while/body/eval_jaxpr/ppermute | solution.py:11
  83.4 11.4 %collective-permute-start.2 = (f32[16,32]{0,1:T(8,128)S(1)}, f32[16,32]{0,1:T(8,128)S(1)}, u32[]{:S(2)}, u32[]{:S(2)}) collective-permute-start(f32[16,32]{0,1:T(8,128)S(1)} %get-tuple-element.564), channel_id=1, source_target_pairs={{0,1},{1,2},{2,3},{3,4},{4,5},{5,6},{6,7},{7,0},{8,9},{9,10},{10,1... | collective-permute-start | bytes 6152 | tf_op jit(solution)/shard_map/while/body/eval_jaxpr/ppermute | solution.py:11
  83.4 11.5 %collective-permute-start.3 = (f32[16,32]{0,1:T(8,128)S(1)}, f32[16,32]{0,1:T(8,128)S(1)}, u32[]{:S(2)}, u32[]{:S(2)}) collective-permute-start(f32[16,32]{0,1:T(8,128)S(1)} %get-tuple-element.565), channel_id=1, source_target_pairs={{0,1},{1,2},{2,3},{3,4},{4,5},{5,6},{6,7},{7,0},{8,9},{9,10},{10,1... | collective-permute-start | bytes 6152 | tf_op jit(solution)/shard_map/while/body/eval_jaxpr/ppermute | solution.py:11
  99.3 10.9 %collective-permute-start.1 = (f32[16,4096]{1,0:T(8,128)S(1)}, f32[16,4096]{1,0:T(8,128)S(1)}, u32[]{:S(2)}, u32[]{:S(2)}) collective-permute-start(f32[16,4096]{1,0:T(8,128)S(1)} %fusion.72), channel_id=1, source_target_pairs={{0,1},{1,2},{2,3},{3,4},{4,5},{5,6},{6,7},{7,0},{8,9},{9,10},{10,1... | collective-permute-start | bytes 786440 | tf_op jit(solution)/shard_map/while/body/eval_jaxpr/ppermute | solution.py:11
  99.3 10.8 %collective-permute-start = (bf16[16,4096]{1,0:T(8,128)(2,1)S(1)}, bf16[16,4096]{1,0:T(8,128)(2,1)S(1)}, u32[]{:S(2)}, u32[]{:S(2)}) collective-permute-start(bf16[16,4096]{1,0:T(8,128)(2,1)S(1)} %copy.144), channel_id=1, source_target_pairs={{0,1},{1,2},{2,3},{3,4},{4,5},{5,6},{6,7},{7,0},{8,9},{9,10},{10,1... | collective-permute-start | bytes 393224 | tf_op jit(solution)/shard_map/while/body/eval_jaxpr/ppermute | solution.py:11
  99.4 10.6 %collective-permute-start.2 = (f32[16,32]{0,1:T(8,128)S(1)}, f32[16,32]{0,1:T(8,128)S(1)}, u32[]{:S(2)}, u32[]{:S(2)}) collective-permute-start(f32[16,32]{0,1:T(8,128)S(1)} %get-tuple-element.564), channel_id=1, source_target_pairs={{0,1},{1,2},{2,3},{3,4},{4,5},{5,6},{6,7},{7,0},{8,9},{9,10},{10,1... | collective-permute-start | bytes 6152 | tf_op jit(solution)/shard_map/while/body/eval_jaxpr/ppermute | solution.py:11
  99.5 10.7 %collective-permute-start.3 = (f32[16,32]{0,1:T(8,128)S(1)}, f32[16,32]{0,1:T(8,128)S(1)}, u32[]{:S(2)}, u32[]{:S(2)}) collective-permute-start(f32[16,32]{0,1:T(8,128)S(1)} %get-tuple-element.565), channel_id=1, source_target_pairs={{0,1},{1,2},{2,3},{3,4},{4,5},{5,6},{6,7},{7,0},{8,9},{9,10},{10,1... | collective-permute-start | bytes 6152 | tf_op jit(solution)/shard_map/while/body/eval_jaxpr/ppermute | solution.py:11
  114.5 10.9 %collective-permute-start.1 = (f32[16,4096]{1,0:T(8,128)S(1)}, f32[16,4096]{1,0:T(8,128)S(1)}, u32[]{:S(2)}, u32[]{:S(2)}) collective-permute-start(f32[16,4096]{1,0:T(8,128)S(1)} %fusion.72), channel_id=1, source_target_pairs={{0,1},{1,2},{2,3},{3,4},{4,5},{5,6},{6,7},{7,0},{8,9},{9,10},{10,1... | collective-permute-start | bytes 786440 | tf_op jit(solution)/shard_map/while/body/eval_jaxpr/ppermute | solution.py:11
  114.6 10.8 %collective-permute-start = (bf16[16,4096]{1,0:T(8,128)(2,1)S(1)}, bf16[16,4096]{1,0:T(8,128)(2,1)S(1)}, u32[]{:S(2)}, u32[]{:S(2)}) collective-permute-start(bf16[16,4096]{1,0:T(8,128)(2,1)S(1)} %copy.144), channel_id=1, source_target_pairs={{0,1},{1,2},{2,3},{3,4},{4,5},{5,6},{6,7},{7,0},{8,9},{9,10},{10,1... | collective-permute-start | bytes 393224 | tf_op jit(solution)/shard_map/while/body/eval_jaxpr/ppermute | solution.py:11
  114.7 10.6 %collective-permute-start.2 = (f32[16,32]{0,1:T(8,128)S(1)}, f32[16,32]{0,1:T(8,128)S(1)}, u32[]{:S(2)}, u32[]{:S(2)}) collective-permute-start(f32[16,32]{0,1:T(8,128)S(1)} %get-tuple-element.564), channel_id=1, source_target_pairs={{0,1},{1,2},{2,3},{3,4},{4,5},{5,6},{6,7},{7,0},{8,9},{9,10},{10,1... | collective-permute-start | bytes 6152 | tf_op jit(solution)/shard_map/while/body/eval_jaxpr/ppermute | solution.py:11
  114.7 10.7 %collective-permute-start.3 = (f32[16,32]{0,1:T(8,128)S(1)}, f32[16,32]{0,1:T(8,128)S(1)}, u32[]{:S(2)}, u32[]{:S(2)}) collective-permute-start(f32[16,32]{0,1:T(8,128)S(1)} %get-tuple-element.565), channel_id=1, source_target_pairs={{0,1},{1,2},{2,3},{3,4},{4,5},{5,6},{6,7},{7,0},{8,9},{9,10},{10,1... | collective-permute-start | bytes 6152 | tf_op jit(solution)/shard_map/while/body/eval_jaxpr/ppermute | solution.py:11
  129.8 10.9 %collective-permute-start.1 = (f32[16,4096]{1,0:T(8,128)S(1)}, f32[16,4096]{1,0:T(8,128)S(1)}, u32[]{:S(2)}, u32[]{:S(2)}) collective-permute-start(f32[16,4096]{1,0:T(8,128)S(1)} %fusion.72), channel_id=1, source_target_pairs={{0,1},{1,2},{2,3},{3,4},{4,5},{5,6},{6,7},{7,0},{8,9},{9,10},{10,1... | collective-permute-start | bytes 786440 | tf_op jit(solution)/shard_map/while/body/eval_jaxpr/ppermute | solution.py:11
  129.9 10.8 %collective-permute-start = (bf16[16,4096]{1,0:T(8,128)(2,1)S(1)}, bf16[16,4096]{1,0:T(8,128)(2,1)S(1)}, u32[]{:S(2)}, u32[]{:S(2)}) collective-permute-start(bf16[16,4096]{1,0:T(8,128)(2,1)S(1)} %copy.144), channel_id=1, source_target_pairs={{0,1},{1,2},{2,3},{3,4},{4,5},{5,6},{6,7},{7,0},{8,9},{9,10},{10,1... | collective-permute-start | bytes 393224 | tf_op jit(solution)/shard_map/while/body/eval_jaxpr/ppermute | solution.py:11
  129.9 10.6 %collective-permute-start.2 = (f32[16,32]{0,1:T(8,128)S(1)}, f32[16,32]{0,1:T(8,128)S(1)}, u32[]{:S(2)}, u32[]{:S(2)}) collective-permute-start(f32[16,32]{0,1:T(8,128)S(1)} %get-tuple-element.564), channel_id=1, source_target_pairs={{0,1},{1,2},{2,3},{3,4},{4,5},{5,6},{6,7},{7,0},{8,9},{9,10},{10,1... | collective-permute-start | bytes 6152 | tf_op jit(solution)/shard_map/while/body/eval_jaxpr/ppermute | solution.py:11
  130.0 10.7 %collective-permute-start.3 = (f32[16,32]{0,1:T(8,128)S(1)}, f32[16,32]{0,1:T(8,128)S(1)}, u32[]{:S(2)}, u32[]{:S(2)}) collective-permute-start(f32[16,32]{0,1:T(8,128)S(1)} %get-tuple-element.565), channel_id=1, source_target_pairs={{0,1},{1,2},{2,3},{3,4},{4,5},{5,6},{6,7},{7,0},{8,9},{9,10},{10,1... | collective-permute-start | bytes 6152 | tf_op jit(solution)/shard_map/while/body/eval_jaxpr/ppermute | solution.py:11
  142.9 9.4 %collective-permute-start.4 = (f32[16,4096]{1,0:T(8,128)S(1)}, f32[16,4096]{1,0:T(8,128)S(1)}, u32[]{:S(2)}, u32[]{:S(2)}) collective-permute-start(f32[16,4096]{1,0:T(8,128)S(1)} %fusion.39), channel_id=1, source_target_pairs={{0,1},{1,2},{2,3},{3,4},{4,5},{5,6},{6,7},{7,0},{8,9},{9,10},{10,1... | collective-permute-start | bytes 786440 | tf_op jit(solution)/shard_map/ppermute | solution.py:11
  143.6 8.6 %collective-permute-start.5 = (f32[16,32]{0,1:T(8,128)S(1)}, f32[16,32]{0,1:T(8,128)S(1)}, u32[]{:S(2)}, u32[]{:S(2)}) collective-permute-start(f32[16,32]{0,1:T(8,128)S(1)} %get-tuple-element.404), channel_id=1, source_target_pairs={{0,1},{1,2},{2,3},{3,4},{4,5},{5,6},{6,7},{7,0},{8,9},{9,10},{10,1... | collective-permute-start | bytes 6152 | tf_op jit(solution)/shard_map/ppermute | solution.py:11
where the time goes:
time: 165 us
  waiting for transfers between devices  83.6 us (51%)
  starting transfers between devices  27.9 us (17%)
  local copies, waits for them, and re-layouts  16 us (10%)
  other arithmetic  14 us (8%)
  blocking collectives  8.17 us (5%)
  matrix products  6.6 us (4%)
  loops' own time  5.46 us (3%)
  between operations  2.83 us (2%)
    ppermute x30, waiting for transfers between devices, shifted(): lax.ppermute(value, axis, [(i, (i + by) % length) for i in range(length)])  76.3 us
    ppermute x30, starting transfers between devices, shifted(): lax.ppermute(value, axis, [(i, (i + by) % length) for i in range(length)])  16.9 us
    all_to_all x1, blocking collectives, local(): lax.all_to_all(blended[None], 'grp', split_axis=1, concat_axis=0, tiled=T...  8.17 us
    another operation x1, loops' own time, local(): lax.fori_loop(0, members - 1, cycle_turn, (local_q, start))  5.46 us
    dynamic_slice x8, local copies, waits for them, and re-layouts, visit_block(): query_pos = block_order[source] * row_count + query_lane  5.17 us
    lt x8, other arithmetic, allowed_for(): cache_ok = block_index * cached + cache_lane < hit_limit  4.57 us
    all_to_all x1, starting transfers between devices, local(): lax.all_to_all(new_keys, 'grp', split_axis=0, concat_axis=1, tiled=True)  4.26 us
    all_to_all x1, waiting for transfers between devices, local(): lax.all_to_all(queries, 'grp', split_axis=0, concat_axis=1, tiled=True)  3.68 us
  transfers between devices with their start and end apart: 33, of which 17 were waited for; matrix products, arithmetic and copies ran while one was open for 2% of the time, Pallas kernels for 0%

commit v1 on v0

--- a/solution.py
+++ b/solution.py
@@ -113,7 +113,12 @@
         row_count, full_width
     )
     blended = jnp.where((own_pos < filled)[:, None], blended, 0.0).astype(jnp.bfloat16)
-    return lax.all_to_all(blended[None], "grp", split_axis=1, concat_axis=0, tiled=True)
+    return jnp.concatenate(
+        lax.all_to_all(
+            jnp.stack(jnp.split(blended[None], lax.axis_size("grp"), axis=1)), "grp", 0, 0
+        ),
+        axis=0,
+    )
 
 
 def solution(mesh):

time: 165 us -> 162 us (0.982)
  local copies, waits for them, and re-layouts: 16 us -> 14 us
where the time goes in v1:
time: 162 us; the launch traced here: 161 us
  waiting for transfers between devices  83.6 us (52%)
  starting transfers between devices  27.9 us (17%)
  local copies, waits for them, and re-layouts  14 us (9%)
  other arithmetic  12.7 us (8%)
  blocking collectives  8.2 us (5%)
  matrix products  6.61 us (4%)
  loops' own time  5.44 us (3%)
  between operations  2.89 us (2%)
    ppermute x30, waiting for transfers between devices, shifted(): lax.ppermute(value, axis, [(i, (i + by) % length) for i in range(length)])  76.2 us
    ppermute x30, starting transfers between devices, shifted(): lax.ppermute(value, axis, [(i, (i + by) % length) for i in range(length)])  16.9 us
    all_to_all x1, blocking collectives, local(): lax.all_to_all(jnp.stack(jnp.split(blended[None], lax.axis_size('grp'), a...  8.2 us
    another operation x1, loops' own time, local(): lax.fori_loop(0, members - 1, cycle_turn, (local_q, start))  5.44 us
    dynamic_slice x8, local copies, waits for them, and re-layouts, visit_block(): query_pos = block_order[source] * row_count + query_lane  4.91 us
    lt x8, other arithmetic, allowed_for(): cache_ok = block_index * cached + cache_lane < hit_limit  4.57 us
    all_to_all x1, starting transfers between devices, local(): lax.all_to_all(new_keys, 'grp', split_axis=0, concat_axis=1, tiled=True)  4.26 us
    all_to_all x1, waiting for transfers between devices, local(): lax.all_to_all(queries, 'grp', split_axis=0, concat_axis=1, tiled=True)  3.68 us
  transfers between devices with their start and end apart: 33, of which 17 were waited for; matrix products, arithmetic and copies ran while one was open for 2% of the time, Pallas kernels for 0%

profile of v1, /device:TPU:0, one launch (start us, length us, event | category | flops | bytes accessed | tf_op | source)
XLA Modules:
  0.0 161.4 jit_solution(6893438910517770208)
XLA Ops:
  0.0 4.3 %all-to-all-start.1 = ((bf16[4,4,512]{2,1,0:T(4,128)(2,1)}), bf16[4,4,512]{2,1,0:T(4,128)(2,1)S(1)}, u32[]{:S(2)}, u32[]{:S(2)}) async-start(bf16[4,4,512]{2,1,0:T(4,128)(2,1)} %param.13), calls=%async_computation.1 | async-start | bytes 32768 | tf_op jit(solution)/shard_map/all_to_all | solution.py:55
  4.3 0.7 copy-done.5
  4.9 0.6 constant_dynamic-slice_fusion
  7.7 1.1 concatenate.36
  8.8 0.9 copy.27
  10.1 3.4 %all-to-all-start.2 = ((bf16[4,4,512]{2,1,0:T(4,128)(2,1)}), bf16[4,4,512]{2,1,0:T(4,128)(2,1)S(1)}, u32[]{:S(2)}, u32[]{:S(2)}) async-start(bf16[4,4,512]{2,1,0:T(4,128)(2,1)} %param.14), calls=%async_computation.2 | async-start | bytes 32768 | tf_op jit(solution)/shard_map/all_to_all | solution.py:56
  13.8 3.7 %all-to-all-done.2 = bf16[4,4,512]{2,1,0:T(4,128)(2,1)S(1)} async-done(((bf16[4,4,512]{2,1,0:T(4,128)(2,1)}), bf16[4,4,512]{2,1,0:T(4,128)(2,1)S(1)}, u32[]{:S(2)}, u32[]{:S(2)}) %all-to-all-start.2) | async-done | bytes 16416 | tf_op jit(solution)/shard_map/all_to_all | solution.py:56
  17.4 3.3 %all-to-all-start = ((bf16[4,4,4096]{2,1,0:T(4,128)(2,1)}), bf16[4,4,4096]{2,1,0:T(4,128)(2,1)S(1)}, u32[]{:S(2)}, u32[]{:S(2)}) async-start(bf16[4,4,4096]{2,1,0:T(4,128)(2,1)} %param.10), calls=%async_computation | async-start | bytes 262144 | tf_op jit(solution)/shard_map/all_to_all | solution.py:54
  21.0 0.6 copy-done.1
  21.7 3.7 %all-to-all-done = bf16[4,4,4096]{2,1,0:T(4,128)(2,1)S(1)} async-done(((bf16[4,4,4096]{2,1,0:T(4,128)(2,1)}), bf16[4,4,4096]{2,1,0:T(4,128)(2,1)S(1)}, u32[]{:S(2)}, u32[]{:S(2)}) %all-to-all-start) | async-done | bytes 131104 | tf_op jit(solution)/shard_map/all_to_all | solution.py:54
  25.4 115.0 %while.24 = (s32[]{:T(128)}, bf16[16,4096]{1,0:T(8,128)(2,1)S(1)}, f32[16,4096]{1,0:T(8,128)S(1)}, f32[16,32]{0,1:T(8,128)S(1)}, f32[16,32]{0,1:T(8,128)S(1)}, /...) while((s32[]{:T(128)}, bf16[16,4096]{1,0:T(8,128)(2,1)S(1)}, ...), condition=%wide.wide.region_3.4_spmd.clone.clone, body=%wide.wide.region_0.3_spmd.clone.clone.sunk | while | flops 124177328 | bytes 8742969 | solution.py:109
  25.5 0.6 dynamic_slice.32
  26.9 0.7 fusion.68
  27.6 0.4 fusion.69
  29.3 0.5 fusion.72
  29.8 2.0 %collective-permute-start.1 = (f32[16,4096]{1,0:T(8,128)S(1)}, f32[16,4096]{1,0:T(8,128)S(1)}, u32[]{:S(2)}, u32[]{:S(2)}) collective-permute-start(f32[16,4096]{1,0:T(8,128)S(1)} %fusion.72), channel_id=1, source_target_pairs={{0,1},{1,2},{2,3},{3,4},{4,5},{5,6},{6,7},{7,0},{8,9},{9,10},{10,1... | collective-permute-start | bytes 786440 | tf_op jit(solution)/shard_map/while/body/eval_jaxpr/ppermute | solution.py:11
  31.8 1.6 collective-permute-start
  33.3 1.5 collective-permute-start.2
  34.8 1.6 collective-permute-start.3
  36.4 7.7 %collective-permute-done.2 = f32[16,32]{0,1:T(8,128)S(1)} collective-permute-done((f32[16,32]{0,1:T(8,128)S(1)}, f32[16,32]{0,1:T(8,128)S(1)}, u32[]{:S(2)}, u32[]{:S(2)}) %collective-permute-start.2) | collective-permute-done | bytes 2080 | tf_op jit(solution)/shard_map/while/body/eval_jaxpr/ppermute | solution.py:11
  44.3 0.6 dynamic_slice.32
  45.7 0.7 fusion.68
  46.4 0.4 fusion.69
  48.1 0.5 fusion.72
  48.7 1.1 collective-permute-start
  49.8 0.6 collective-permute-start.2
  50.4 2.4 %collective-permute-start.3 = (f32[16,32]{0,1:T(8,128)S(1)}, f32[16,32]{0,1:T(8,128)S(1)}, u32[]{:S(2)}, u32[]{:S(2)}) collective-permute-start(f32[16,32]{0,1:T(8,128)S(1)} %get-tuple-element.569), channel_id=1, source_target_pairs={{0,1},{1,2},{2,3},{3,4},{4,5},{5,6},{6,7},{7,0},{8,9},{9,10},{10,1... | collective-permute-start | bytes 6152 | tf_op jit(solution)/shard_map/while/body/eval_jaxpr/ppermute | solution.py:11
  52.9 8.9 %collective-permute-done.2 = f32[16,32]{0,1:T(8,128)S(1)} collective-permute-done((f32[16,32]{0,1:T(8,128)S(1)}, f32[16,32]{0,1:T(8,128)S(1)}, u32[]{:S(2)}, u32[]{:S(2)}) %collective-permute-start.2) | collective-permute-done | bytes 2080 | tf_op jit(solution)/shard_map/while/body/eval_jaxpr/ppermute | solution.py:11
  62.0 0.6 dynamic_slice.32
  63.4 0.7 fusion.68
  64.1 0.4 fusion.69
  65.8 0.5 fusion.72
  66.5 2.0 %collective-permute-start.3 = (f32[16,32]{0,1:T(8,128)S(1)}, f32[16,32]{0,1:T(8,128)S(1)}, u32[]{:S(2)}, u32[]{:S(2)}) collective-permute-start(f32[16,32]{0,1:T(8,128)S(1)} %get-tuple-element.569), channel_id=1, source_target_pairs={{0,1},{1,2},{2,3},{3,4},{4,5},{5,6},{6,7},{7,0},{8,9},{9,10},{10,1... | collective-permute-start | bytes 6152 | tf_op jit(solution)/shard_map/while/body/eval_jaxpr/ppermute | solution.py:11
  68.5 10.2 %collective-permute-done.2 = f32[16,32]{0,1:T(8,128)S(1)} collective-permute-done((f32[16,32]{0,1:T(8,128)S(1)}, f32[16,32]{0,1:T(8,128)S(1)}, u32[]{:S(2)}, u32[]{:S(2)}) %collective-permute-start.2) | collective-permute-done | bytes 2080 | tf_op jit(solution)/shard_map/while/body/eval_jaxpr/ppermute | solution.py:11
  78.9 0.6 dynamic_slice.32
  80.2 0.7 fusion.68
  81.0 0.4 fusion.69
  82.7 0.5 fusion.72
  83.4 11.2 %collective-permute-done.2 = f32[16,32]{0,1:T(8,128)S(1)} collective-permute-done((f32[16,32]{0,1:T(8,128)S(1)}, f32[16,32]{0,1:T(8,128)S(1)}, u32[]{:S(2)}, u32[]{:S(2)}) %collective-permute-start.2) | collective-permute-done | bytes 2080 | tf_op jit(solution)/shard_map/while/body/eval_jaxpr/ppermute | solution.py:11
  94.9 0.6 dynamic_slice.32
  96.2 0.7 fusion.68
  97.0 0.4 fusion.69
  98.7 0.5 fusion.72
  99.3 0.5 collective-permute-start.3
  99.8 10.0 %collective-permute-done.2 = f32[16,32]{0,1:T(8,128)S(1)} collective-permute-done((f32[16,32]{0,1:T(8,128)S(1)}, f32[16,32]{0,1:T(8,128)S(1)}, u32[]{:S(2)}, u32[]{:S(2)}) %collective-permute-start.2) | collective-permute-done | bytes 2080 | tf_op jit(solution)/shard_map/while/body/eval_jaxpr/ppermute | solution.py:11
  110.1 0.6 dynamic_slice.32
  111.4 0.7 fusion.68
  112.2 0.4 fusion.69
  113.0 0.4 fusion.71
  113.9 0.5 fusion.72
  114.6 1.3 collective-permute-start.3
  115.8 9.2 %collective-permute-done.2 = f32[16,32]{0,1:T(8,128)S(1)} collective-permute-done((f32[16,32]{0,1:T(8,128)S(1)}, f32[16,32]{0,1:T(8,128)S(1)}, u32[]{:S(2)}, u32[]{:S(2)}) %collective-permute-start.2) | collective-permute-done | bytes 2080 | tf_op jit(solution)/shard_map/while/body/eval_jaxpr/ppermute | solution.py:11
  125.3 0.6 dynamic_slice.32
  126.6 0.7 fusion.68
  127.4 0.4 fusion.69
  128.2 0.4 fusion.71
  129.1 0.5 fusion.72
  129.8 1.3 collective-permute-start.3
  131.1 9.2 %collective-permute-done.2 = f32[16,32]{0,1:T(8,128)S(1)} collective-permute-done((f32[16,32]{0,1:T(8,128)S(1)}, f32[16,32]{0,1:T(8,128)S(1)}, u32[]{:S(2)}, u32[]{:S(2)}) %collective-permute-start.2) | collective-permute-done | bytes 2080 | tf_op jit(solution)/shard_map/while/body/eval_jaxpr/ppermute | solution.py:11
  140.5 0.4 fusion.51
  142.2 0.5 fusion.39
  143.4 8.5 %collective-permute-done.5 = f32[16,32]{0,1:T(8,128)S(1)} collective-permute-done((f32[16,32]{0,1:T(8,128)S(1)}, f32[16,32]{0,1:T(8,128)S(1)}, u32[]{:S(2)}, u32[]{:S(2)}) %collective-permute-start.5) | collective-permute-done | bytes 2080 | tf_op jit(solution)/shard_map/ppermute | solution.py:11
  152.5 8.2 %all_to_all.32 = bf16[4,1,4,4096]{3,2,1,0:T(4,128)(2,1)S(1)} all-to-all(bf16[4,1,4,4096]{3,2,1,0:T(4,128)(2,1)S(1)} %pad_maximum_fusion.2), channel_id=1, replica_groups=mesh['grp'=4,'blk'=8] {'grp'}, dimensions={0} | all-to-all | bytes 262144 | tf_op jit(solution)/shard_map/all_to_all | solution.py:117
  160.7 0.7 copy.124
  (199 shorter events, 14.3 us)
Async XLA Ops:
  0.0 10.1 %all-to-all-start.1 = ((bf16[4,4,512]{2,1,0:T(4,128)(2,1)}), bf16[4,4,512]{2,1,0:T(4,128)(2,1)S(1)}, u32[]{:S(2)}, u32[]{:S(2)}) async-start(bf16[4,4,512]{2,1,0:T(4,128)(2,1)} %param.13), calls=%async_computation.1 | async-start | bytes 32768 | tf_op jit(solution)/shard_map/all_to_all | solution.py:55
  4.3 0.7 copy-start.5
  8.8 1.1 copy-start.3
  10.0 3.5 %copy-start.2 = (bf16[1,448,512]{2,1,0:T(8,128)(2,1)S(1)}, bf16[1,448,512]{2,1,0:T(8,128)(2,1)}, u32[]{:S(2)}) copy-start(bf16[1,448,512]{2,1,0:T(8,128)(2,1)} %param.11) | copy-start | bytes 1376260
  10.1 7.3 %all-to-all-start.2 = ((bf16[4,4,512]{2,1,0:T(4,128)(2,1)}), bf16[4,4,512]{2,1,0:T(4,128)(2,1)S(1)}, u32[]{:S(2)}, u32[]{:S(2)}) async-start(bf16[4,4,512]{2,1,0:T(4,128)(2,1)} %param.14), calls=%async_computation.2 | async-start | bytes 32768 | tf_op jit(solution)/shard_map/all_to_all | solution.py:56
  13.6 3.8 %copy-start = (bf16[464,512]{1,0:T(8,128)(2,1)}, bf16[464,512]{1,0:T(8,128)(2,1)S(1)}, u32[]{:S(2)}) copy-start(bf16[464,512]{1,0:T(8,128)(2,1)S(1)} %pad_maximum_fusion) | copy-start | bytes 1425412
  17.4 7.9 %all-to-all-start = ((bf16[4,4,4096]{2,1,0:T(4,128)(2,1)}), bf16[4,4,4096]{2,1,0:T(4,128)(2,1)S(1)}, u32[]{:S(2)}, u32[]{:S(2)}) async-start(bf16[4,4,4096]{2,1,0:T(4,128)(2,1)} %param.10), calls=%async_computation | async-start | bytes 262144 | tf_op jit(solution)/shard_map/all_to_all | solution.py:54
  20.8 0.8 copy-start.1
  25.4 115.1 %copy-start.4 = (bf16[448,4,128]{2,0,1:T(8,128)(2,1)S(1)}, bf16[448,4,128]{2,0,1:T(8,128)(2,1)}, u32[]{:S(2)}) copy-start(bf16[448,4,128]{2,0,1:T(8,128)(2,1)} %copy.27) | copy-start | bytes 1376260
  29.8 14.5 %collective-permute-start.1 = (f32[16,4096]{1,0:T(8,128)S(1)}, f32[16,4096]{1,0:T(8,128)S(1)}, u32[]{:S(2)}, u32[]{:S(2)}) collective-permute-start(f32[16,4096]{1,0:T(8,128)S(1)} %fusion.72), channel_id=1, source_target_pairs={{0,1},{1,2},{2,3},{3,4},{4,5},{5,6},{6,7},{7,0},{8,9},{9,10},{10,1... | collective-permute-start | bytes 786440 | tf_op jit(solution)/shard_map/while/body/eval_jaxpr/ppermute | solution.py:11
  31.8 12.5 %collective-permute-start = (bf16[16,4096]{1,0:T(8,128)(2,1)S(1)}, bf16[16,4096]{1,0:T(8,128)(2,1)S(1)}, u32[]{:S(2)}, u32[]{:S(2)}) collective-permute-start(bf16[16,4096]{1,0:T(8,128)(2,1)S(1)} %copy.112), channel_id=1, source_target_pairs={{0,1},{1,2},{2,3},{3,4},{4,5},{5,6},{6,7},{7,0},{8,9},{9,10},{10,1... | collective-permute-start | bytes 393224 | tf_op jit(solution)/shard_map/while/body/eval_jaxpr/ppermute | solution.py:11
  33.3 10.8 %collective-permute-start.2 = (f32[16,32]{0,1:T(8,128)S(1)}, f32[16,32]{0,1:T(8,128)S(1)}, u32[]{:S(2)}, u32[]{:S(2)}) collective-permute-start(f32[16,32]{0,1:T(8,128)S(1)} %get-tuple-element.568), channel_id=1, source_target_pairs={{0,1},{1,2},{2,3},{3,4},{4,5},{5,6},{6,7},{7,0},{8,9},{9,10},{10,1... | collective-permute-start | bytes 6152 | tf_op jit(solution)/shard_map/while/body/eval_jaxpr/ppermute | solution.py:11
  34.8 9.4 %collective-permute-start.3 = (f32[16,32]{0,1:T(8,128)S(1)}, f32[16,32]{0,1:T(8,128)S(1)}, u32[]{:S(2)}, u32[]{:S(2)}) collective-permute-start(f32[16,32]{0,1:T(8,128)S(1)} %get-tuple-element.569), channel_id=1, source_target_pairs={{0,1},{1,2},{2,3},{3,4},{4,5},{5,6},{6,7},{7,0},{8,9},{9,10},{10,1... | collective-permute-start | bytes 6152 | tf_op jit(solution)/shard_map/while/body/eval_jaxpr/ppermute | solution.py:11
  48.6 13.4 %collective-permute-start.1 = (f32[16,4096]{1,0:T(8,128)S(1)}, f32[16,4096]{1,0:T(8,128)S(1)}, u32[]{:S(2)}, u32[]{:S(2)}) collective-permute-start(f32[16,4096]{1,0:T(8,128)S(1)} %fusion.72), channel_id=1, source_target_pairs={{0,1},{1,2},{2,3},{3,4},{4,5},{5,6},{6,7},{7,0},{8,9},{9,10},{10,1... | collective-permute-start | bytes 786440 | tf_op jit(solution)/shard_map/while/body/eval_jaxpr/ppermute | solution.py:11
  48.7 13.3 %collective-permute-start = (bf16[16,4096]{1,0:T(8,128)(2,1)S(1)}, bf16[16,4096]{1,0:T(8,128)(2,1)S(1)}, u32[]{:S(2)}, u32[]{:S(2)}) collective-permute-start(bf16[16,4096]{1,0:T(8,128)(2,1)S(1)} %copy.112), channel_id=1, source_target_pairs={{0,1},{1,2},{2,3},{3,4},{4,5},{5,6},{6,7},{7,0},{8,9},{9,10},{10,1... | collective-permute-start | bytes 393224 | tf_op jit(solution)/shard_map/while/body/eval_jaxpr/ppermute | solution.py:11
  49.8 12.0 %collective-permute-start.2 = (f32[16,32]{0,1:T(8,128)S(1)}, f32[16,32]{0,1:T(8,128)S(1)}, u32[]{:S(2)}, u32[]{:S(2)}) collective-permute-start(f32[16,32]{0,1:T(8,128)S(1)} %get-tuple-element.568), channel_id=1, source_target_pairs={{0,1},{1,2},{2,3},{3,4},{4,5},{5,6},{6,7},{7,0},{8,9},{9,10},{10,1... | collective-permute-start | bytes 6152 | tf_op jit(solution)/shard_map/while/body/eval_jaxpr/ppermute | solution.py:11
  50.4 11.6 %collective-permute-start.3 = (f32[16,32]{0,1:T(8,128)S(1)}, f32[16,32]{0,1:T(8,128)S(1)}, u32[]{:S(2)}, u32[]{:S(2)}) collective-permute-start(f32[16,32]{0,1:T(8,128)S(1)} %get-tuple-element.569), channel_id=1, source_target_pairs={{0,1},{1,2},{2,3},{3,4},{4,5},{5,6},{6,7},{7,0},{8,9},{9,10},{10,1... | collective-permute-start | bytes 6152 | tf_op jit(solution)/shard_map/while/body/eval_jaxpr/ppermute | solution.py:11
  66.3 12.5 %collective-permute-start.1 = (f32[16,4096]{1,0:T(8,128)S(1)}, f32[16,4096]{1,0:T(8,128)S(1)}, u32[]{:S(2)}, u32[]{:S(2)}) collective-permute-start(f32[16,4096]{1,0:T(8,128)S(1)} %fusion.72), channel_id=1, source_target_pairs={{0,1},{1,2},{2,3},{3,4},{4,5},{5,6},{6,7},{7,0},{8,9},{9,10},{10,1... | collective-permute-start | bytes 786440 | tf_op jit(solution)/shard_map/while/body/eval_jaxpr/ppermute | solution.py:11
  66.4 12.4 %collective-permute-start = (bf16[16,4096]{1,0:T(8,128)(2,1)S(1)}, bf16[16,4096]{1,0:T(8,128)(2,1)S(1)}, u32[]{:S(2)}, u32[]{:S(2)}) collective-permute-start(bf16[16,4096]{1,0:T(8,128)(2,1)S(1)} %copy.112), channel_id=1, source_target_pairs={{0,1},{1,2},{2,3},{3,4},{4,5},{5,6},{6,7},{7,0},{8,9},{9,10},{10,1... | collective-permute-start | bytes 393224 | tf_op jit(solution)/shard_map/while/body/eval_jaxpr/ppermute | solution.py:11
  66.4 12.2 %collective-permute-start.2 = (f32[16,32]{0,1:T(8,128)S(1)}, f32[16,32]{0,1:T(8,128)S(1)}, u32[]{:S(2)}, u32[]{:S(2)}) collective-permute-start(f32[16,32]{0,1:T(8,128)S(1)} %get-tuple-element.568), channel_id=1, source_target_pairs={{0,1},{1,2},{2,3},{3,4},{4,5},{5,6},{6,7},{7,0},{8,9},{9,10},{10,1... | collective-permute-start | bytes 6152 | tf_op jit(solution)/shard_map/while/body/eval_jaxpr/ppermute | solution.py:11
  66.5 12.3 %collective-permute-start.3 = (f32[16,32]{0,1:T(8,128)S(1)}, f32[16,32]{0,1:T(8,128)S(1)}, u32[]{:S(2)}, u32[]{:S(2)}) collective-permute-start(f32[16,32]{0,1:T(8,128)S(1)} %get-tuple-element.569), channel_id=1, source_target_pairs={{0,1},{1,2},{2,3},{3,4},{4,5},{5,6},{6,7},{7,0},{8,9},{9,10},{10,1... | collective-permute-start | bytes 6152 | tf_op jit(solution)/shard_map/while/body/eval_jaxpr/ppermute | solution.py:11
  83.2 11.6 %collective-permute-start.1 = (f32[16,4096]{1,0:T(8,128)S(1)}, f32[16,4096]{1,0:T(8,128)S(1)}, u32[]{:S(2)}, u32[]{:S(2)}) collective-permute-start(f32[16,4096]{1,0:T(8,128)S(1)} %fusion.72), channel_id=1, source_target_pairs={{0,1},{1,2},{2,3},{3,4},{4,5},{5,6},{6,7},{7,0},{8,9},{9,10},{10,1... | collective-permute-start | bytes 786440 | tf_op jit(solution)/shard_map/while/body/eval_jaxpr/ppermute | solution.py:11
  83.2 11.6 %collective-permute-start = (bf16[16,4096]{1,0:T(8,128)(2,1)S(1)}, bf16[16,4096]{1,0:T(8,128)(2,1)S(1)}, u32[]{:S(2)}, u32[]{:S(2)}) collective-permute-start(bf16[16,4096]{1,0:T(8,128)(2,1)S(1)} %copy.112), channel_id=1, source_target_pairs={{0,1},{1,2},{2,3},{3,4},{4,5},{5,6},{6,7},{7,0},{8,9},{9,10},{10,1... | collective-permute-start | bytes 393224 | tf_op jit(solution)/shard_map/while/body/eval_jaxpr/ppermute | solution.py:11
  83.3 11.3 %collective-permute-start.2 = (f32[16,32]{0,1:T(8,128)S(1)}, f32[16,32]{0,1:T(8,128)S(1)}, u32[]{:S(2)}, u32[]{:S(2)}) collective-permute-start(f32[16,32]{0,1:T(8,128)S(1)} %get-tuple-element.568), channel_id=1, source_target_pairs={{0,1},{1,2},{2,3},{3,4},{4,5},{5,6},{6,7},{7,0},{8,9},{9,10},{10,1... | collective-permute-start | bytes 6152 | tf_op jit(solution)/shard_map/while/body/eval_jaxpr/ppermute | solution.py:11
  83.4 11.4 %collective-permute-start.3 = (f32[16,32]{0,1:T(8,128)S(1)}, f32[16,32]{0,1:T(8,128)S(1)}, u32[]{:S(2)}, u32[]{:S(2)}) collective-permute-start(f32[16,32]{0,1:T(8,128)S(1)} %get-tuple-element.569), channel_id=1, source_target_pairs={{0,1},{1,2},{2,3},{3,4},{4,5},{5,6},{6,7},{7,0},{8,9},{9,10},{10,1... | collective-permute-start | bytes 6152 | tf_op jit(solution)/shard_map/while/body/eval_jaxpr/ppermute | solution.py:11
  99.1 10.9 %collective-permute-start.1 = (f32[16,4096]{1,0:T(8,128)S(1)}, f32[16,4096]{1,0:T(8,128)S(1)}, u32[]{:S(2)}, u32[]{:S(2)}) collective-permute-start(f32[16,4096]{1,0:T(8,128)S(1)} %fusion.72), channel_id=1, source_target_pairs={{0,1},{1,2},{2,3},{3,4},{4,5},{5,6},{6,7},{7,0},{8,9},{9,10},{10,1... | collective-permute-start | bytes 786440 | tf_op jit(solution)/shard_map/while/body/eval_jaxpr/ppermute | solution.py:11
  99.2 10.8 %collective-permute-start = (bf16[16,4096]{1,0:T(8,128)(2,1)S(1)}, bf16[16,4096]{1,0:T(8,128)(2,1)S(1)}, u32[]{:S(2)}, u32[]{:S(2)}) collective-permute-start(bf16[16,4096]{1,0:T(8,128)(2,1)S(1)} %copy.112), channel_id=1, source_target_pairs={{0,1},{1,2},{2,3},{3,4},{4,5},{5,6},{6,7},{7,0},{8,9},{9,10},{10,1... | collective-permute-start | bytes 393224 | tf_op jit(solution)/shard_map/while/body/eval_jaxpr/ppermute | solution.py:11
  99.3 10.6 %collective-permute-start.2 = (f32[16,32]{0,1:T(8,128)S(1)}, f32[16,32]{0,1:T(8,128)S(1)}, u32[]{:S(2)}, u32[]{:S(2)}) collective-permute-start(f32[16,32]{0,1:T(8,128)S(1)} %get-tuple-element.568), channel_id=1, source_target_pairs={{0,1},{1,2},{2,3},{3,4},{4,5},{5,6},{6,7},{7,0},{8,9},{9,10},{10,1... | collective-permute-start | bytes 6152 | tf_op jit(solution)/shard_map/while/body/eval_jaxpr/ppermute | solution.py:11
  99.3 10.7 %collective-permute-start.3 = (f32[16,32]{0,1:T(8,128)S(1)}, f32[16,32]{0,1:T(8,128)S(1)}, u32[]{:S(2)}, u32[]{:S(2)}) collective-permute-start(f32[16,32]{0,1:T(8,128)S(1)} %get-tuple-element.569), channel_id=1, source_target_pairs={{0,1},{1,2},{2,3},{3,4},{4,5},{5,6},{6,7},{7,0},{8,9},{9,10},{10,1... | collective-permute-start | bytes 6152 | tf_op jit(solution)/shard_map/while/body/eval_jaxpr/ppermute | solution.py:11
  114.4 10.9 %collective-permute-start.1 = (f32[16,4096]{1,0:T(8,128)S(1)}, f32[16,4096]{1,0:T(8,128)S(1)}, u32[]{:S(2)}, u32[]{:S(2)}) collective-permute-start(f32[16,4096]{1,0:T(8,128)S(1)} %fusion.72), channel_id=1, source_target_pairs={{0,1},{1,2},{2,3},{3,4},{4,5},{5,6},{6,7},{7,0},{8,9},{9,10},{10,1... | collective-permute-start | bytes 786440 | tf_op jit(solution)/shard_map/while/body/eval_jaxpr/ppermute | solution.py:11
  114.4 10.8 %collective-permute-start = (bf16[16,4096]{1,0:T(8,128)(2,1)S(1)}, bf16[16,4096]{1,0:T(8,128)(2,1)S(1)}, u32[]{:S(2)}, u32[]{:S(2)}) collective-permute-start(bf16[16,4096]{1,0:T(8,128)(2,1)S(1)} %copy.112), channel_id=1, source_target_pairs={{0,1},{1,2},{2,3},{3,4},{4,5},{5,6},{6,7},{7,0},{8,9},{9,10},{10,1... | collective-permute-start | bytes 393224 | tf_op jit(solution)/shard_map/while/body/eval_jaxpr/ppermute | solution.py:11
  114.5 10.6 %collective-permute-start.2 = (f32[16,32]{0,1:T(8,128)S(1)}, f32[16,32]{0,1:T(8,128)S(1)}, u32[]{:S(2)}, u32[]{:S(2)}) collective-permute-start(f32[16,32]{0,1:T(8,128)S(1)} %get-tuple-element.568), channel_id=1, source_target_pairs={{0,1},{1,2},{2,3},{3,4},{4,5},{5,6},{6,7},{7,0},{8,9},{9,10},{10,1... | collective-permute-start | bytes 6152 | tf_op jit(solution)/shard_map/while/body/eval_jaxpr/ppermute | solution.py:11
  114.6 10.7 %collective-permute-start.3 = (f32[16,32]{0,1:T(8,128)S(1)}, f32[16,32]{0,1:T(8,128)S(1)}, u32[]{:S(2)}, u32[]{:S(2)}) collective-permute-start(f32[16,32]{0,1:T(8,128)S(1)} %get-tuple-element.569), channel_id=1, source_target_pairs={{0,1},{1,2},{2,3},{3,4},{4,5},{5,6},{6,7},{7,0},{8,9},{9,10},{10,1... | collective-permute-start | bytes 6152 | tf_op jit(solution)/shard_map/while/body/eval_jaxpr/ppermute | solution.py:11
  129.6 10.9 %collective-permute-start.1 = (f32[16,4096]{1,0:T(8,128)S(1)}, f32[16,4096]{1,0:T(8,128)S(1)}, u32[]{:S(2)}, u32[]{:S(2)}) collective-permute-start(f32[16,4096]{1,0:T(8,128)S(1)} %fusion.72), channel_id=1, source_target_pairs={{0,1},{1,2},{2,3},{3,4},{4,5},{5,6},{6,7},{7,0},{8,9},{9,10},{10,1... | collective-permute-start | bytes 786440 | tf_op jit(solution)/shard_map/while/body/eval_jaxpr/ppermute | solution.py:11
  129.6 10.8 %collective-permute-start = (bf16[16,4096]{1,0:T(8,128)(2,1)S(1)}, bf16[16,4096]{1,0:T(8,128)(2,1)S(1)}, u32[]{:S(2)}, u32[]{:S(2)}) collective-permute-start(bf16[16,4096]{1,0:T(8,128)(2,1)S(1)} %copy.112), channel_id=1, source_target_pairs={{0,1},{1,2},{2,3},{3,4},{4,5},{5,6},{6,7},{7,0},{8,9},{9,10},{10,1... | collective-permute-start | bytes 393224 | tf_op jit(solution)/shard_map/while/body/eval_jaxpr/ppermute | solution.py:11
  129.7 10.6 %collective-permute-start.2 = (f32[16,32]{0,1:T(8,128)S(1)}, f32[16,32]{0,1:T(8,128)S(1)}, u32[]{:S(2)}, u32[]{:S(2)}) collective-permute-start(f32[16,32]{0,1:T(8,128)S(1)} %get-tuple-element.568), channel_id=1, source_target_pairs={{0,1},{1,2},{2,3},{3,4},{4,5},{5,6},{6,7},{7,0},{8,9},{9,10},{10,1... | collective-permute-start | bytes 6152 | tf_op jit(solution)/shard_map/while/body/eval_jaxpr/ppermute | solution.py:11
  129.8 10.7 %collective-permute-start.3 = (f32[16,32]{0,1:T(8,128)S(1)}, f32[16,32]{0,1:T(8,128)S(1)}, u32[]{:S(2)}, u32[]{:S(2)}) collective-permute-start(f32[16,32]{0,1:T(8,128)S(1)} %get-tuple-element.569), channel_id=1, source_target_pairs={{0,1},{1,2},{2,3},{3,4},{4,5},{5,6},{6,7},{7,0},{8,9},{9,10},{10,1... | collective-permute-start | bytes 6152 | tf_op jit(solution)/shard_map/while/body/eval_jaxpr/ppermute | solution.py:11
  142.7 9.4 %collective-permute-start.4 = (f32[16,4096]{1,0:T(8,128)S(1)}, f32[16,4096]{1,0:T(8,128)S(1)}, u32[]{:S(2)}, u32[]{:S(2)}) collective-permute-start(f32[16,4096]{1,0:T(8,128)S(1)} %fusion.39), channel_id=1, source_target_pairs={{0,1},{1,2},{2,3},{3,4},{4,5},{5,6},{6,7},{7,0},{8,9},{9,10},{10,1... | collective-permute-start | bytes 786440 | tf_op jit(solution)/shard_map/ppermute | solution.py:11
  143.4 8.6 %collective-permute-start.5 = (f32[16,32]{0,1:T(8,128)S(1)}, f32[16,32]{0,1:T(8,128)S(1)}, u32[]{:S(2)}, u32[]{:S(2)}) collective-permute-start(f32[16,32]{0,1:T(8,128)S(1)} %get-tuple-element.404), channel_id=1, source_target_pairs={{0,1},{1,2},{2,3},{3,4},{4,5},{5,6},{6,7},{7,0},{8,9},{9,10},{10,1... | collective-permute-start | bytes 6152 | tf_op jit(solution)/shard_map/ppermute | solution.py:11
